TPU v7x, 512 devices: a whole 4x4x16 slice. The times are simulated.
512 devices in a mesh: gx: 16 (over z_lo, core), gy: 32 (over x, z_hi, y).
Axes of the slice: x: 4, y: 4, z: 16 (z_hi: 2, z_lo: 8; z = z_hi * 8 + z_lo), core: 2. Of those that a mesh axis runs over, the one named last changes fastest.
Arguments:
- field: float32 [5, 1, 512, 4096], P(None, None, 'gx', 'gy'), may hold values from -6 to 6
- cotangent: float32 [5, 1, 512, 4096], P(None, None, 'gx', 'gy'), may hold values from -6 to 6
- lift: float32 [15, 32], replicated, may hold values from -1.5 to 1.5
- spectral: float32 [2, 2, 64, 32, 32], replicated, may hold values from -6 to 6
- pointwise: float32 [2, 32, 32], replicated, may hold values from -1 to 1
- project: float32 [32, 5], replicated, may hold values from -1 to 1
Outputs:
- field_grad: float32 [5, 1, 512, 4096], P(None, None, 'gx', 'gy')
All inputs are finite; a program needn't handle non-finite values.
Results may differ from a plain program's by a relative error of at most 0.0003.
Values sent between devices are 32-bit elements; how exact they have to be, the bound alone decides.
A program may use at most 64 MiB of HBM per device.

v0:
```python
import functools
import math

import jax
import jax.numpy as jnp
import numpy as np
from jax import lax
from jax.experimental import pallas as pl
from jax.experimental.pallas import tpu as pltpu
from jax.sharding import PartitionSpec as P

F32, BF16 = jnp.float32, jnp.bfloat16
LOOP = False
ROWS, COLS, W, CIN, MD = 32, 128, 32, 16, 8
WAVES = [(0, 0), (1, 0), (1, 1), (2, 0), (2, 1), (3, 0), (3, 1), (4, 0), (4, 1)]
NWAVE = len(WAVES)
HIGHEST = lax.Precision.HIGHEST


def mode_waves():
    j = np.arange(COLS)[:, None]
    kx = np.repeat(np.arange(MD) - MD // 2, MD)[None, :]
    ky = np.tile(np.arange(MD), MD)[None, :]
    b = 2 * np.pi * ((j * ky) % COLS) / COLS
    scale = 1.0 / math.sqrt(ROWS * COLS)
    parts = []
    for k, is_sin in WAVES:
        hit = (np.abs(kx) == k).astype(np.float64)
        if is_sin:
            sg = np.sign(kx) * hit
            re, im = -sg * np.sin(b), -sg * np.cos(b)
        else:
            re, im = hit * np.cos(b), -hit * np.sin(b)
        parts.append(np.concatenate([re, im], axis=1) * scale)
    table = np.concatenate(parts, axis=0).astype(np.float32)
    hi = table.astype(jnp.bfloat16)
    lo = (table - hi.astype(np.float32)).astype(jnp.bfloat16)
    return np.concatenate([hi, lo], axis=1)


def wave(k, i):
    return math.cos(2 * math.pi * k * i / ROWS), math.sin(2 * math.pi * k * i / ROWS)


def weighted(terms):
    total = None
    for c, x in terms:
        if abs(c) < 1e-12:
            continue
        t = x if abs(c - 1) < 1e-12 else (-x if abs(c + 1) < 1e-12 else x * np.float32(c))
        total = t if total is None else total + t
    return total


def tree_sum(xs):
    xs = list(xs)
    while len(xs) > 1:
        xs = [xs[i] + xs[i + 1] if i + 1 < len(xs) else xs[i] for i in range(0, len(xs), 2)]
    return xs[0]


def to_waves(x):
    s = [x[i] + x[i + 16] for i in range(16)]
    d = [x[i] - x[i + 16] for i in range(16)]
    dc = [d[0]] + [d[i] - d[16 - i] for i in range(1, 8)]
    ds = [None] + [d[i] + d[16 - i] for i in range(1, 8)] + [d[8]]
    out = {}
    for k in (1, 3):
        out[(k, 0)] = weighted([(wave(k, i)[0], dc[i]) for i in range(8)])
        out[(k, 1)] = weighted([(wave(k, i)[1], ds[i]) for i in range(1, 9)])
    p = [s[i] + s[i + 8] for i in range(8)]
    m = [s[i] - s[i + 8] for i in range(8)]
    mc = [m[0]] + [m[i] - m[8 - i] for i in range(1, 4)]
    ms = [None] + [m[i] + m[8 - i] for i in range(1, 4)] + [m[4]]
    out[(2, 0)] = weighted([(wave(2, i)[0], mc[i]) for i in range(4)])
    out[(2, 1)] = weighted([(wave(2, i)[1], ms[i]) for i in range(1, 5)])
    q = [p[i] - p[i + 4] for i in range(4)]
    r = np.float32(math.sqrt(0.5))
    out[(4, 0)] = q[0] + r * (q[1] - q[3])
    out[(4, 1)] = q[2] + r * (q[1] + q[3])
    out[(0, 0)] = tree_sum([p[i] + p[i + 4] for i in range(4)])
    return [out[w] for w in WAVES]


def to_rows(a):
    a = dict(zip(WAVES, a))
    r = np.float32(math.sqrt(0.5))
    c0, c4, s4 = a[(0, 0)], a[(4, 0)], a[(4, 1)]
    u, v = r * (c4 + s4), r * (s4 - c4)
    e04 = [c0 + c4, c0 + u, c0 + s4, c0 + v, c0 - c4, c0 - u, c0 - s4, c0 - v]
    c2 = [weighted([(wave(2, i)[0], a[(2, 0)])]) for i in range(4)]
    s2 = [None] + [weighted([(wave(2, i)[1], a[(2, 1)])]) for i in range(1, 5)]
    e2 = [c2[0]] + [c2[i] + s2[i] for i in range(1, 4)] + [s2[4]] + [s2[8 - i] - c2[8 - i] for i in range(5, 8)]
    ev = [e04[i] + e2[i] for i in range(8)] + [e04[i] - e2[i] for i in range(8)]
    oc = [weighted([(wave(k, i)[0], a[(k, 0)]) for k in (1, 3)]) for i in range(8)]
    os_ = [None] + [weighted([(wave(k, i)[1], a[(k, 1)]) for k in (1, 3)]) for i in range(1, 9)]
    od = [oc[0]] + [oc[i] + os_[i] for i in range(1, 8)] + [os_[8]] + [os_[16 - i] - oc[16 - i] for i in range(9, 16)]
    return [ev[i] + od[i] for i in range(16)] + [ev[i] - od[i] for i in range(16)]


def split(x):
    hi = x.astype(BF16)
    lo = (x - hi.astype(F32)).astype(BF16)
    return hi, lo


def tall(x):
    hi, lo = split(x)
    return jnp.concatenate([hi, lo, hi], axis=0)


def wide(x):
    hi, lo = split(x)
    return jnp.concatenate([hi, hi, lo], axis=1)


def channel_mix(left, x_ref, width, out_ref, out_width):
    for i in range(0, ROWS, 2):
        right = jnp.concatenate([tall(x_ref[(i + t) * width:(i + t + 1) * width, :]) for t in range(2)], axis=1)
        got = jnp.dot(left, right, preferred_element_type=F32)
        out_ref[i * out_width:(i + 1) * out_width, :] = got[:, :COLS]
        out_ref[(i + 1) * out_width:(i + 2) * out_width, :] = got[:, COLS:]


def each_group(width, fn):
    if LOOP:
        @pl.loop(0, width // 8)
        def _(n):
            fn(pl.multiple_of(n * 8, 8))
    else:
        for g in range(0, width, 8):
            fn(g)


def analyse(x_ref, width, g_ref, waves_ref):
    def group(g):
        got = to_waves([x_ref[pl.ds(i * width + g, 8), :] for i in range(ROWS)])
        for n in range(NWAVE):
            g_ref[pl.ds(g, 8), n * COLS:(n + 1) * COLS] = got[n]
    each_group(width, group)
    hi, lo = split(g_ref[0:width, :])
    both = jnp.dot(jnp.concatenate([hi, lo], axis=0), waves_ref[...], preferred_element_type=F32)
    return (both[:width, :COLS] + both[width:, :COLS]) + (both[:width, COLS:] + both[width:, COLS:])


def synthesise(coef, width, a_ref, waves_ref):
    hi, lo = split(coef)
    left = jnp.concatenate([jnp.concatenate([hi, hi], axis=1), jnp.concatenate([lo, lo], axis=1)], axis=0)
    both = lax.dot_general(left, waves_ref[...], (((1,), (1,)), ((), ())), preferred_element_type=F32)
    a_ref[0:width, :] = both[:width] + both[width:]


def waves_of(a_ref, g):
    return [a_ref[pl.ds(g, 8), n * COLS:(n + 1) * COLS] for n in range(NWAVE)]


def half_swap(x):
    return jnp.concatenate([x[:, 64:], x[:, :64]], axis=1)


def mix_modes(coef, wr_ref, wi_ref, layer, c_ref):
    c_ref[0:W, :] = coef
    c_ref[W:2 * W, :] = half_swap(coef)
    accs = [None] * 4
    for w in range(W):
        t = (wr_ref[layer, w] * jnp.broadcast_to(c_ref[w:w + 1, :], (W, COLS))
             + wi_ref[layer, w] * jnp.broadcast_to(c_ref[W + w:W + w + 1, :], (W, COLS)))
        accs[w % 4] = t if accs[w % 4] is None else accs[w % 4] + t
    return (accs[0] + accs[1]) + (accs[2] + accs[3])


def unmix_modes(grad, wr_ref, wi_ref, layer, r_ref):
    swapped = half_swap(grad)
    for w in range(W):
        t = wr_ref[layer, w] * grad - wi_ref[layer, w] * swapped
        r_ref[w * 8:(w + 1) * 8, :] = (t[0:8] + t[8:16]) + (t[16:24] + t[24:32])
    return tree_sum([r_ref[pl.ds(s, W, stride=8), :] for s in range(8)])


def gelu_parts(x):
    cdf = 0.5 * lax.erf(x * np.float32(math.sqrt(0.5))) + 0.5
    pdf = jnp.exp(-0.5 * (x * x)) * np.float32(1.0 / math.sqrt(2 * math.pi))
    return x * cdf, cdf + x * pdf


def prepare(spectral_ref, wr_ref, wi_ref):
    for layer in range(2):
        for w in range(W):
            re, im = spectral_ref[layer, 0, w], spectral_ref[layer, 1, w]
            wr_ref[layer, w] = jnp.concatenate([re, re], axis=1)
            wi_ref[layer, w] = jnp.concatenate([-im, im], axis=1)


def network_grad(f_ref, cot_ref, lift_ref, spectral_ref, point_ref, proj_ref, waves_ref, out_ref, scr, prep=True):
    wr, wi, g, a, c, r, pw, h, d1, pc = scr
    if prep:
        prepare(spectral_ref, wr, wi)
    lift16 = jnp.concatenate([lift_ref[...], jnp.zeros((1, W), F32)], axis=0)
    p1, p2 = point_ref[0], point_ref[1]
    both1 = jnp.dot(lift16, p1, precision=HIGHEST, preferred_element_type=F32)
    both1_t = jnp.transpose(both1)
    lift_t = jnp.transpose(lift16)
    proj8 = jnp.concatenate([proj_ref[...], jnp.zeros((3, W), F32)], axis=0)
    proj_t = jnp.transpose(proj8)
    channel_mix(wide(proj_t), cot_ref, 8, pc, W)
    channel_mix(wide(both1_t), f_ref, CIN, pw, W)
    coef = analyse(f_ref, CIN, g, waves_ref)
    coef = jnp.dot(lift_t, coef, precision=HIGHEST, preferred_element_type=F32)
    synthesise(mix_modes(coef, wr, wi, 0, c), W, a, waves_ref)
    def group1(gr):
        rows = to_rows(waves_of(a, gr))
        for i in range(ROWS):
            sl = pl.ds(i * W + gr, 8)
            val, der = gelu_parts(rows[i] + pw[sl, :])
            h[sl, :] = val
            d1[sl, :] = der
    each_group(W, group1)
    channel_mix(wide(jnp.transpose(p2)), h, W, pw, W)
    coef = analyse(h, W, g, waves_ref)
    synthesise(mix_modes(coef, wr, wi, 1, c), W, a, waves_ref)
    def group2(gr):
        rows = to_rows(waves_of(a, gr))
        for i in range(ROWS):
            sl = pl.ds(i * W + gr, 8)
            _, der = gelu_parts(rows[i] + pw[sl, :])
            h[sl, :] = der * pc[sl, :]
    each_group(W, group2)
    channel_mix(wide(p2), h, W, pw, W)
    coef = analyse(h, W, g, waves_ref)
    synthesise(unmix_modes(coef, wr, wi, 1, r), W, a, waves_ref)
    def group3(gr):
        rows = to_rows(waves_of(a, gr))
        for i in range(ROWS):
            sl = pl.ds(i * W + gr, 8)
            h[sl, :] = d1[sl, :] * (rows[i] + pw[sl, :])
    each_group(W, group3)
    channel_mix(wide(both1), h, W, pw, CIN)
    coef = analyse(h, W, g, waves_ref)
    coef = unmix_modes(coef, wr, wi, 0, r)
    coef = jnp.dot(lift16, coef, precision=HIGHEST, preferred_element_type=F32)
    synthesise(coef, CIN, a, waves_ref)
    def group4(gr):
        rows = to_rows(waves_of(a, gr))
        for i in range(ROWS):
            sl = pl.ds(i * CIN + gr, 8)
            out_ref[sl, :] = rows[i] + pw[sl, :]
    each_group(CIN, group4)


VARS = 5
TILE = 8
MESH = pl.DeviceIdType.MESH
AROUND = sorted(
    ((dx, dy) for dx in range(-2, 3) for dy in range(-2, 3) if (dx, dy) != (0, 0)),
    key=lambda o: (o[1] == 0, abs(o[1]), abs(o[0]), o),
)


def tiles_of(dx, dy):
    if abs(dx) == 2 or abs(dy) == 2:
        return 1
    return VARS if dx == 0 or dy == 0 else 3


START = {}
TILES = 0
for _o in AROUND:
    START[_o] = TILES
    TILES += tiles_of(*_o)


def pieces(dx, dy):
    out = []
    far_col, near_col = 0, 32 if dy == -1 else 0
    blocks = {-1: (1,), 0: (0, 1), 1: (0,)}[dx]
    for ch in range(VARS):
        if dx == 0:
            for rb in blocks:
                out.append(("near", ch, rb, near_col, 32, ch, 32 * rb))
            out.append(("far", ch, 0, far_col, 32, ch, 64))
        elif dy == 0:
            out.append(("near", ch, blocks[0], 0, 64, ch, 0))
            out.append(("far", ch, 0, 0, 32, ch, 64))
        else:
            base = 64 * (ch % 2)
            out.append(("near", ch, blocks[0], near_col, 32, ch // 2, base))
            out.append(("far", ch, 0, far_col, 32, ch // 2, base + 32))
    return out


def far_edge_col(dy):
    return 16 if dy == -2 else 0


def near_lane(col, dy=0):
    return 32 + col + 64 * dy


def far_lane(col, dy=0):
    return 48 + col + 32 * dy


FAR_ROW = {-2: 0, -1: 4, 0: 12, 1: 20, 2: 28}


def lane_ids():
    return lax.broadcasted_iota(jnp.int32, (TILE, COLS), 1)


def row_ids():
    return lax.broadcasted_iota(jnp.int32, (TILE, COLS), 0)


def turned(x, shift, axis=1, period=None):
    shift %= period or x.shape[axis]
    return x if shift == 0 else pltpu.roll(x, shift, axis)


class Lanes:
    def __init__(self):
        self.lane = lane_ids()
        self.row = row_ids()
        self.masks = {}

    def mask(self, first, width):
        key = (first, width)
        if key not in self.masks:
            self.masks[key] = (self.lane >= first) & (self.lane < first + width)
        return self.masks[key]

    def put(self, base, value, first, width):
        return value if base is None else jnp.where(self.mask(first, width), value, base)

    def only(self, value, first, width):
        return jnp.where(self.mask(first, width), value, 0.0)


def pool_maps():
    j = np.arange(COLS)[:, None]
    lane = np.arange(COLS)[None, :]
    gather = np.concatenate(
        [((lane - 32) % 64 == j // 2) * 0.25, ((lane - 48) % 32 == j // 4) * 0.0625], axis=1
    )
    spread = np.concatenate(
        [(j - 32 == lane // 2) * 0.25, (j - 48 == lane // 4) * 0.0625], axis=1
    )
    return np.concatenate([gather, spread], axis=0).astype(jnp.bfloat16)


def mapped(rows, table):
    hi, lo = split(rows)
    both = jnp.dot(jnp.concatenate([hi, lo], axis=0), table, preferred_element_type=F32)
    return both[: rows.shape[0]] + both[rows.shape[0]:]


def send_tiles(lanes, near, far, buf):
    rolled = {}

    def near_at(ch, rb, col, lane):
        key = ("n", ch, rb, (lane - near_lane(col)) % 64)
        if key not in rolled:
            rolled[key] = turned(near[ch][rb], key[3], period=64)
        return rolled[key]

    def far_at(ch, col, lane):
        key = ("f", ch, (lane - far_lane(col)) % 32)
        if key not in rolled:
            rolled[key] = turned(far[ch], key[2], period=32)
        return rolled[key]

    strips = {}
    for dx, dy in AROUND:
        start = START[dx, dy]
        if abs(dy) == 2:
            if ("y", dy) not in strips:
                tile = None
                for ch in range(VARS):
                    tile = lanes.put(tile, far_at(ch, far_edge_col(dy), 16 * ch), 16 * ch, 16)
                strips["y", dy] = tile
            buf[start * TILE:(start + 1) * TILE, :] = strips["y", dy]
        elif abs(dx) == 2:
            if ("x", dx) not in strips:
                tile = None
                for ch in range(4):
                    tile = lanes.put(tile, far_at(ch, 0, 32 * ch), 32 * ch, 32)
                last = far_at(4, 0, 0)
                if dx == -2:
                    tile = turned(tile, 4, axis=0)
                else:
                    last = turned(last, 4, axis=0)
                strips["x", dx] = jnp.where(lanes.mask(0, 32) & (lanes.row >= 4), last, tile)
            buf[start * TILE:(start + 1) * TILE, :] = strips["x", dx]
        else:
            tiles = [None] * tiles_of(dx, dy)
            for kind, ch, rb, col, width, tile, lane in pieces(dx, dy):
                value = near_at(ch, rb, col, lane) if kind == "near" else far_at(ch, col, lane)
                tiles[tile] = lanes.put(tiles[tile], value, lane, width)
            for n, value in enumerate(tiles):
                buf[(start + n) * TILE:(start + n + 1) * TILE, :] = value


def tile_at(buf, o, n=0):
    first = (START[o] + n) * TILE
    return buf[first:first + TILE, :]


def read_windows(lanes, near, far, buf, f_ref):
    blocks = {}
    rows = {}
    for ch in range(VARS):
        blocks[ch, 1], blocks[ch, 2] = near[ch]
        rows[ch, 0] = far[ch]
    for dx in (0, -1, 1):
        for dy in (0, -1, 1):
            if (dx, dy) == (0, 0):
                continue
            for kind, ch, rb, col, width, tile, lane in pieces(dx, dy):
                value = tile_at(buf, (dx, dy), tile)
                if kind == "near":
                    key = (ch, {-1: 0, 0: 1 + rb, 1: 3}[dx])
                    to, table = near_lane(col, dy), blocks
                else:
                    key, to, table = (ch, dx), far_lane(col, dy), rows
                table[key] = lanes.put(table.get(key), turned(value, to - lane), to, width)
    for dx in (-2, 2):
        for dy in (0, -1, 1):
            value = tile_at(buf, (dx, dy))
            low = turned(value, 4, axis=0)
            for ch in range(VARS):
                to, lane = far_lane(0, dy), 32 * ch if ch < 4 else 0
                got = turned(value if ch < 4 else low, to - lane)
                rows[ch, dx] = lanes.put(rows.get((ch, dx)), got, to, 32)
    for dx in range(-2, 3):
        for dy in (-2, 2):
            value = tile_at(buf, (dx, dy))
            if dx == -2:
                value = turned(value, 4, axis=0)
            for ch in range(VARS):
                to = far_lane(far_edge_col(dy), dy)
                rows[ch, dx] = lanes.put(rows[ch, dx], turned(value, to - 16 * ch), to, 16)
    for (ch, k), value in blocks.items():
        f_ref[pl.ds(8 * k * CIN + VARS + ch, TILE, stride=CIN), :] = value
    for (ch, dx), value in rows.items():
        count = 4 if abs(dx) == 2 else TILE
        f_ref[pl.ds(FAR_ROW[dx] * CIN + 2 * VARS + ch, count, stride=CIN), :] = value[:count]


def window_tiles(go):
    near = {(ch, k): go[pl.ds(8 * k * CIN + VARS + ch, TILE, stride=CIN), :] for ch in range(VARS) for k in range(4)}
    far = {}
    for ch in range(VARS):
        for dx in range(-2, 3):
            first = 24 if dx == 2 else FAR_ROW[dx]
            far[ch, dx] = go[pl.ds(first * CIN + 2 * VARS + ch, TILE, stride=CIN), :]
    return near, far


def send_grads(lanes, near, far, buf):
    for dx, dy in AROUND:
        start = START[dx, dy]
        if abs(dy) == 2:
            tile = None
            for ch in range(VARS):
                got = turned(far[ch, dx], 16 * ch - far_lane(far_edge_col(dy), dy))
                tile = lanes.put(tile, got, 16 * ch, 16)
            if abs(dx) == 2:
                tile = turned(tile, 4, axis=0)
                keep = lanes.row >= 4 if dx == -2 else lanes.row < 4
                tile = jnp.where(keep, tile, 0.0)
            buf[start * TILE:(start + 1) * TILE, :] = tile
        elif abs(dx) == 2:
            tile = None
            for ch in range(4):
                tile = lanes.put(tile, turned(far[ch, dx], 32 * ch - far_lane(0, dy)), 32 * ch, 32)
            last = turned(far[4, dx], -far_lane(0, dy))
            if dx == -2:
                last = turned(last, 4, axis=0)
            else:
                tile = turned(tile, 4, axis=0)
            buf[start * TILE:(start + 1) * TILE, :] = jnp.where(lanes.mask(0, 32) & (lanes.row >= 4), last, tile)
        else:
            tiles = [None] * tiles_of(dx, dy)
            for kind, ch, rb, col, width, tile, lane in pieces(dx, dy):
                if kind == "near":
                    value = turned(near[ch, {-1: 0, 0: 1 + rb, 1: 3}[dx]], lane - near_lane(col, dy))
                else:
                    value = turned(far[ch, dx], lane - far_lane(col, dy))
                tiles[tile] = lanes.put(tiles[tile], value, lane, width)
            for n, value in enumerate(tiles):
                buf[(start + n) * TILE:(start + n + 1) * TILE, :] = value


def sum_grads(lanes, near, far, buf):
    n_sum = {(ch, rb): lanes.only(near[ch, 1 + rb], 32, 64) for ch in range(VARS) for rb in range(2)}
    f_sum = {ch: lanes.only(far[ch, 0], 48, 32) for ch in range(VARS)}
    for dx in (-1, 0, 1):
        for dy in (-1, 0, 1):
            if (dx, dy) == (0, 0):
                continue
            for kind, ch, rb, col, width, tile, lane in pieces(dx, dy):
                value = tile_at(buf, (dx, dy), tile)
                if kind == "near":
                    to = near_lane(col)
                    n_sum[ch, rb] += lanes.only(turned(value, to - lane), to, width)
                else:
                    to = far_lane(col)
                    f_sum[ch] += lanes.only(turned(value, to - lane), to, width)
    for dx in (-2, 2):
        value = tree_sum([tile_at(buf, (dx, dy)) for dy in (-1, 0, 1)])
        low = turned(value, 4, axis=0)
        keep = lanes.row >= 4 if dx == -2 else lanes.row < 4
        for ch in range(VARS):
            natural = (ch < 4) == (dx == 2)
            lane = 32 * ch if ch < 4 else 0
            got = turned(value if natural else low, far_lane(0) - lane)
            f_sum[ch] += jnp.where(lanes.mask(48, 32) & keep, got, 0.0)
    for dy in (-2, 2):
        value = tree_sum([tile_at(buf, (dx, dy)) for dx in range(-2, 3)])
        for ch in range(VARS):
            to = far_lane(far_edge_col(dy))
            f_sum[ch] += lanes.only(turned(value, to - 16 * ch), to, 16)
    return (
        jnp.concatenate([n_sum[ch, rb] for ch in range(VARS) for rb in range(2)], axis=0),
        jnp.concatenate([f_sum[ch] for ch in range(VARS)], axis=0),
    )


def kernel(counts, field_hbm, cot_hbm, lift_hbm, spectral_hbm, point_hbm, proj_hbm, waves_hbm, maps_hbm, out_ref,
           field, cot, lift, spectral, point, proj, waves, maps, f, ct, go, pooled, spread_near, spread_far,
           fwd_out, fwd_in, bwd_out, bwd_in, load_sem, send_sem, recv_sem, *scr):
    gx, gy = lax.axis_index("gx"), lax.axis_index("gy")
    n_gx, n_gy = counts

    def device(dx, dy):
        return (lax.rem(gx + (dx + n_gx), n_gx), lax.rem(gy + (dy + n_gy), n_gy))

    barrier = pltpu.get_barrier_semaphore()
    for dx, dy in AROUND:
        pl.semaphore_signal(barrier, inc=1, device_id=device(dx, dy), device_id_type=MESH)
    loads = [
        pltpu.make_async_copy(src, dst, load_sem.at[n])
        for n, (src, dst) in enumerate([
            (field_hbm, field), (maps_hbm, maps), (cot_hbm, cot), (lift_hbm, lift), (point_hbm, point),
            (proj_hbm, proj), (spectral_hbm, spectral), (waves_hbm, waves)])
    ]
    for copy in loads:
        copy.start()

    def exchange(turn, src, dst):
        copies = {}
        for n, (dx, dy) in enumerate(AROUND):
            sign = -1 if turn == 0 else 1
            span = pl.ds(START[dx, dy] * TILE, tiles_of(dx, dy) * TILE)
            copies[dx, dy] = pltpu.make_async_remote_copy(
                src_ref=src.at[span], dst_ref=dst.at[span], send_sem=send_sem.at[turn, n], recv_sem=recv_sem.at[turn, n],
                device_id=device(sign * dx, sign * dy), device_id_type=MESH)
            copies[dx, dy].start()
        return copies

    lanes = Lanes()
    loads[0].wait()
    loads[1].wait()
    half = field[pl.ds(0, 80, stride=2), :] + field[pl.ds(1, 80, stride=2), :]
    pooled[...] = half
    quarter = pooled[pl.ds(0, 40, stride=2), :] + pooled[pl.ds(1, 40, stride=2), :]
    got = mapped(jnp.concatenate([half, quarter], axis=0), maps[0:COLS, :])
    near = [[got[ch * 16 + rb * 8:ch * 16 + rb * 8 + 8, :COLS] for rb in range(2)] for ch in range(VARS)]
    far = [got[80 + ch * 8:80 + ch * 8 + 8, COLS:] for ch in range(VARS)]
    send_tiles(lanes, near, far, fwd_out)
    pl.semaphore_wait(barrier, len(AROUND))
    sent = exchange(0, fwd_out, fwd_in)

    for copy in loads[2:]:
        copy.wait()
    f[...] = jnp.zeros_like(f)
    ct[...] = jnp.zeros_like(ct)
    for v in range(VARS):
        f[pl.ds(v, ROWS, stride=CIN), :] = field[v * ROWS:(v + 1) * ROWS, :]
        ct[pl.ds(v, ROWS, stride=8), :] = cot[v * ROWS:(v + 1) * ROWS, :]
    prepare(spectral, scr[0], scr[1])
    for copy in sent.values():
        copy.wait_recv()
    read_windows(lanes, near, far, fwd_in, f)
    network_grad(f, ct, lift, spectral, point, proj, waves, go, scr, prep=False)

    near, far = window_tiles(go)
    send_grads(lanes, near, far, bwd_out)
    back = exchange(1, bwd_out, bwd_in)
    for copy in back.values():
        copy.wait_recv()
    n_sum, f_sum = sum_grads(lanes, near, far, bwd_in)
    got = mapped(jnp.concatenate([n_sum, f_sum], axis=0), maps[COLS:, :])
    for k in range(2):
        spread_near[pl.ds(k, 80, stride=2), :] = got[:80, :COLS]
    for k in range(4):
        spread_far[pl.ds(k, 40, stride=4), :] = got[80:, COLS:]
    for v in range(VARS):
        span = slice(v * ROWS, (v + 1) * ROWS)
        out_ref[span, :] = go[pl.ds(v, ROWS, stride=CIN), :] + spread_near[span, :] + spread_far[span, :]
    for copies in (sent, back):
        for copy in copies.values():
            copy.wait_send()


def body(counts, field, cotangent, lift, spectral, pointwise, project):
    vmem = lambda *shape, dtype=F32: pltpu.VMEM(shape, dtype)
    flat = (VARS * ROWS, COLS)
    hbm = pl.BlockSpec(memory_space=pltpu.MemorySpace.HBM)
    call = pl.pallas_call(
        functools.partial(kernel, counts),
        out_shape=jax.ShapeDtypeStruct(flat, F32),
        in_specs=[hbm] * 8,
        out_specs=pl.BlockSpec(memory_space=pltpu.VMEM),
        scratch_shapes=[
            vmem(*flat), vmem(*flat), vmem(3 * VARS, W), vmem(2, 2, W, W, MD * MD), vmem(2, W, W), vmem(VARS, W),
            vmem(NWAVE * COLS, 2 * COLS, dtype=BF16), vmem(2 * COLS, 2 * COLS, dtype=BF16),
            vmem(ROWS * CIN, COLS), vmem(ROWS * 8, COLS), vmem(ROWS * CIN, COLS),
            vmem(80, COLS), vmem(*flat), vmem(*flat),
            vmem(TILES * TILE, COLS), vmem(TILES * TILE, COLS), vmem(TILES * TILE, COLS), vmem(TILES * TILE, COLS),
            pltpu.SemaphoreType.DMA((8,)), pltpu.SemaphoreType.DMA((2, len(AROUND))),
            pltpu.SemaphoreType.DMA((2, len(AROUND))),
            vmem(2, W, W, COLS), vmem(2, W, W, COLS), vmem(W, NWAVE * COLS), vmem(W, NWAVE * COLS),
            vmem(2 * W, COLS), vmem(W * 8, COLS), vmem(ROWS * W, COLS), vmem(ROWS * W, COLS), vmem(ROWS * W, COLS),
            vmem(ROWS * W, COLS),
        ],
        compiler_params=pltpu.CompilerParams(collective_id=0, has_side_effects=True, vmem_limit_bytes=48 << 20),
        name="patch_grad",
    )
    out = call(
        field.reshape(flat), cotangent.reshape(flat), lift, spectral.transpose(0, 1, 3, 4, 2), pointwise, project.T,
        jnp.asarray(mode_waves()), jnp.asarray(pool_maps()))
    return out.reshape(field.shape)


def solution(mesh):
    counts = (mesh.shape["gx"], mesh.shape["gy"])
    return jax.shard_map(
        functools.partial(body, counts),
        mesh=mesh,
        in_specs=(P(None, None, "gx", "gy"), P(None, None, "gx", "gy"), P(), P(), P(), P()),
        out_specs=P(None, None, "gx", "gy"),
        check_vma=False,
    )
```

profile of v0, /device:TPU:41, one launch (start us, length us, event | category | flops | bytes accessed | tf_op | source)
XLA Modules:
  0.0 60.3 jit_solution(14282324569065031928)
XLA Ops:
  0.0 0.0 copy-start
  0.0 1.6 %copy-done = f32[2,2,64,32,32]{2,4,3,1,0:T(8,128)S(1)} copy-done((f32[2,2,64,32,32]{2,4,3,1,0:T(8,128)S(1)}, f32[2,2,64,32,32]{2,4,3,1,0:T(8,128)}, u32[]{:S(2)}) %copy-start) | copy-done | bytes 1048600
  1.6 0.0 copy-start.1
  1.6 1.1 %copy-done.1 = bf16[1152,256]{1,0:T(8,128)(2,1)S(1)} copy-done((bf16[1152,256]{1,0:T(8,128)(2,1)S(1)}, bf16[1152,256]{1,0:T(8,128)(2,1)}, u32[]{:S(2)}) %copy-start.1) | copy-done | bytes 589848
  2.7 0.0 copy-start.2
  2.7 0.9 %copy-done.2 = bf16[256,256]{1,0:T(8,128)(2,1)S(1)} copy-done((bf16[256,256]{1,0:T(8,128)(2,1)S(1)}, bf16[256,256]{1,0:T(8,128)(2,1)}, u32[]{:S(2)}) %copy-start.2) | copy-done | bytes 131096
  3.6 0.0 copy-start.3
  3.6 0.9 %copy-done.3 = f32[5,1,32,128]{3,2,1,0:T(8,128)S(1)} copy-done((f32[5,1,32,128]{3,2,1,0:T(8,128)S(1)}, f32[5,1,32,128]{3,2,1,0:T(8,128)}, u32[]{:S(2)}) %copy-start.3) | copy-done | bytes 81944
  4.4 0.0 copy-start.4
  4.5 0.9 %copy-done.4 = f32[5,1,32,128]{3,2,1,0:T(8,128)S(1)} copy-done((f32[5,1,32,128]{3,2,1,0:T(8,128)S(1)}, f32[5,1,32,128]{3,2,1,0:T(8,128)}, u32[]{:S(2)}) %copy-start.4) | copy-done | bytes 81944
  5.3 0.0 copy-start.5
  5.3 0.8 %copy-done.5 = f32[2,32,32]{2,1,0:T(8,128)S(1)} copy-done((f32[2,32,32]{2,1,0:T(8,128)S(1)}, f32[2,32,32]{2,1,0:T(8,128)}, u32[]{:S(2)}) %copy-start.5) | copy-done | bytes 8216
  6.1 0.0 copy-start.6
  6.1 0.7 %copy-done.6 = f32[15,32]{1,0:T(8,128)S(1)} copy-done((f32[15,32]{1,0:T(8,128)S(1)}, f32[15,32]{1,0:T(8,128)}, u32[]{:S(2)}) %copy-start.6) | copy-done | bytes 1944
  6.8 0.0 copy-start.7
  6.8 0.7 %copy-done.7 = f32[32,5]{0,1:T(8,128)S(1)} copy-done((f32[32,5]{0,1:T(8,128)S(1)}, f32[32,5]{0,1:T(8,128)}, u32[]{:S(2)}) %copy-start.7) | copy-done | bytes 664
  7.5 52.2 %patch_grad.1 = f32[160,128]{1,0:T(8,128)S(1)} custom-call(f32[160,128]{1,0:T(8,128)S(1)} %bitcast.9, f32[160,128]{1,0:T(8,128)S(1)} %bitcast.10, f32[15,32]{1,0:T(8,128)S(1)} %copy-done.6, f32[2,2,32,32,64]{4,3,2,1,0:T(8,128)S(1)} %bitcast.7, f32[2,32,32]{2,1,0:T(8,128)S(1)} %copy-done.5, f32[5,32]{1,0:T(8,128)S(1)} %bitcast.11, ...), custom_call_target="tpu_custom_call" | custom-call | tf_op jit(solution)/shard_map/patch_grad/pallas_call | solution.py:629
  59.6 0.6 %copy.11 = f32[5,1,32,128]{3,2,1,0:T(8,128)} copy(f32[5,1,32,128]{3,2,1,0:T(8,128)S(1)} %bitcast.8) | data formatting | bytes 163840
Async XLA Ops:
  0.0 1.6 %copy-start = (f32[2,2,64,32,32]{2,4,3,1,0:T(8,128)S(1)}, f32[2,2,64,32,32]{2,4,3,1,0:T(8,128)}, u32[]{:S(2)}) copy-start(f32[2,2,64,32,32]{2,4,3,1,0:T(8,128)} %param.11) | copy-start | bytes 3145732
  1.6 1.1 %copy-start.1 = (bf16[1152,256]{1,0:T(8,128)(2,1)S(1)}, bf16[1152,256]{1,0:T(8,128)(2,1)}, u32[]{:S(2)}) copy-start(bf16[1152,256]{1,0:T(8,128)(2,1)} %constant.4.clone.waves_hbm) | copy-start | bytes 1769476
  2.7 0.9 %copy-start.2 = (bf16[256,256]{1,0:T(8,128)(2,1)S(1)}, bf16[256,256]{1,0:T(8,128)(2,1)}, u32[]{:S(2)}) copy-start(bf16[256,256]{1,0:T(8,128)(2,1)} %constant.5.clone.maps_hbm) | copy-start | bytes 393220
  3.6 0.9 %copy-start.3 = (f32[5,1,32,128]{3,2,1,0:T(8,128)S(1)}, f32[5,1,32,128]{3,2,1,0:T(8,128)}, u32[]{:S(2)}) copy-start(f32[5,1,32,128]{3,2,1,0:T(8,128)} %param.8) | copy-start | bytes 245764
  4.4 0.9 %copy-start.4 = (f32[5,1,32,128]{3,2,1,0:T(8,128)S(1)}, f32[5,1,32,128]{3,2,1,0:T(8,128)}, u32[]{:S(2)}) copy-start(f32[5,1,32,128]{3,2,1,0:T(8,128)} %param.9) | copy-start | bytes 245764
  5.3 0.8 %copy-start.5 = (f32[2,32,32]{2,1,0:T(8,128)S(1)}, f32[2,32,32]{2,1,0:T(8,128)}, u32[]{:S(2)}) copy-start(f32[2,32,32]{2,1,0:T(8,128)} %point_hbm.1) | copy-start | bytes 24580
  6.1 0.7 %copy-start.6 = (f32[15,32]{1,0:T(8,128)S(1)}, f32[15,32]{1,0:T(8,128)}, u32[]{:S(2)}) copy-start(f32[15,32]{1,0:T(8,128)} %lift_hbm.1) | copy-start | bytes 5764
  6.8 0.7 %copy-start.7 = (f32[32,5]{0,1:T(8,128)S(1)}, f32[32,5]{0,1:T(8,128)}, u32[]{:S(2)}) copy-start(f32[32,5]{0,1:T(8,128)} %param.13) | copy-start | bytes 1924
where the time goes:
time: 60.7 us; the launch traced here: 60.3 us
  Pallas kernels  52.2 us (86%)
  local copies, waits for them, and re-layouts  8.11 us (13%)
    pallas_call x1, Pallas kernels, body(): call(field.reshape(flat), cotangent.reshape(flat), lift, spectral.transpo...  52.2 us
    unnamed x17, local copies, waits for them, and re-layouts  8.11 us

commit v1 on v0

--- a/solution.py
+++ b/solution.py
@@ -608,7 +608,7 @@
     hbm = pl.BlockSpec(memory_space=pltpu.MemorySpace.HBM)
     call = pl.pallas_call(
         functools.partial(kernel, counts),
-        out_shape=jax.ShapeDtypeStruct(flat, F32),
+        out_shape=pltpu.VMEM(flat, F32),
         in_specs=[hbm] * 8,
         out_specs=pl.BlockSpec(memory_space=pltpu.VMEM),
         scratch_shapes=[
@@ -623,7 +623,7 @@
             vmem(2 * W, COLS), vmem(W * 8, COLS), vmem(ROWS * W, COLS), vmem(ROWS * W, COLS), vmem(ROWS * W, COLS),
             vmem(ROWS * W, COLS),
         ],
-        compiler_params=pltpu.CompilerParams(collective_id=0, has_side_effects=True, vmem_limit_bytes=48 << 20),
+        compiler_params=pltpu.CompilerParams(collective_id=0, has_side_effects=True, vmem_limit_bytes=55300 << 10),
         name="patch_grad",
     )
     out = call(

time: 60.7 us -> 52.9 us (0.87)
  local copies, waits for them, and re-layouts: 8.11 us -> 0.64 us
    unnamed x17 -> x1, local copies, waits for them, and re-layouts: 8.11 us -> 0.64 us
where the time goes in v1:
time: 52.9 us; the launch traced here: 52.8 us
  Pallas kernels  52.2 us (99%)
  local copies, waits for them, and re-layouts  0.64 us (1%)
    pallas_call x1, Pallas kernels, body(): call(field.reshape(flat), cotangent.reshape(flat), lift, spectral.transpo...  52.2 us

profile of v1, /device:TPU:41, one launch (start us, length us, event | category | flops | bytes accessed | tf_op | source)
XLA Modules:
  0.0 52.8 jit_solution(17974940464647470631)
XLA Ops:
  0.0 52.2 %patch_grad.1 = f32[160,128]{1,0:T(8,128)S(1)} custom-call(f32[160,128]{1,0:T(8,128)} %bitcast.9, f32[160,128]{1,0:T(8,128)} %bitcast.10, f32[15,32]{1,0:T(8,128)} %lift_hbm.1, f32[2,2,32,32,64]{4,3,2,1,0:T(8,128)} %bitcast.8, f32[2,32,32]{2,1,0:T(8,128)} %point_hbm.1, f32[5,32]{1,0:T(8,128)} %bitcast.11, bf16[1152,256]{1,0:T(8,128)(2,1)} %constant.4.clone.waves_hbm, ...), custom_call_target="tpu_custom_call" | custom-call | tf_op jit(solution)/shard_map/patch_grad/pallas_call | solution.py:629
  52.2 0.6 %copy.11 = f32[5,1,32,128]{3,2,1,0:T(8,128)} copy(f32[5,1,32,128]{3,2,1,0:T(8,128)S(1)} %bitcast.7) | data formatting | bytes 163840

commit v2 on v1

--- a/solution.py
+++ b/solution.py
@@ -191,10 +191,8 @@
             wi_ref[layer, w] = jnp.concatenate([-im, im], axis=1)
 
 
-def network_grad(f_ref, cot_ref, lift_ref, spectral_ref, point_ref, proj_ref, waves_ref, out_ref, scr, prep=True):
-    wr, wi, g, a, c, r, pw, h, d1, pc = scr
-    if prep:
-        prepare(spectral_ref, wr, wi)
+def network_setup(cot_ref, lift_ref, spectral_ref, point_ref, proj_ref, scr):
+    prepare(spectral_ref, scr[0], scr[1])
     lift16 = jnp.concatenate([lift_ref[...], jnp.zeros((1, W), F32)], axis=0)
     p1, p2 = point_ref[0], point_ref[1]
     both1 = jnp.dot(lift16, p1, precision=HIGHEST, preferred_element_type=F32)
@@ -202,10 +200,19 @@
     lift_t = jnp.transpose(lift16)
     proj8 = jnp.concatenate([proj_ref[...], jnp.zeros((3, W), F32)], axis=0)
     proj_t = jnp.transpose(proj8)
-    channel_mix(wide(proj_t), cot_ref, 8, pc, W)
-    channel_mix(wide(both1_t), f_ref, CIN, pw, W)
+    channel_mix(wide(proj_t), cot_ref, 8, scr[-1], W)
+    return {
+        "in": wide(both1_t), "out": wide(both1), "point": wide(p2), "point_t": wide(jnp.transpose(p2)),
+        "lift": lift16, "lift_t": lift_t,
+    }
+
+
+def network_grad(f_ref, setup, waves_ref, out_ref, scr):
+    wr, wi, g, a, c, r, pw, h, d1, pc = scr
+    w = setup
+    channel_mix(w["in"], f_ref, CIN, pw, W)
     coef = analyse(f_ref, CIN, g, waves_ref)
-    coef = jnp.dot(lift_t, coef, precision=HIGHEST, preferred_element_type=F32)
+    coef = jnp.dot(w["lift_t"], coef, precision=HIGHEST, preferred_element_type=F32)
     synthesise(mix_modes(coef, wr, wi, 0, c), W, a, waves_ref)
     def group1(gr):
         rows = to_rows(waves_of(a, gr))
@@ -215,7 +222,7 @@
             h[sl, :] = val
             d1[sl, :] = der
     each_group(W, group1)
-    channel_mix(wide(jnp.transpose(p2)), h, W, pw, W)
+    channel_mix(w["point_t"], h, W, pw, W)
     coef = analyse(h, W, g, waves_ref)
     synthesise(mix_modes(coef, wr, wi, 1, c), W, a, waves_ref)
     def group2(gr):
@@ -225,7 +232,7 @@
             _, der = gelu_parts(rows[i] + pw[sl, :])
             h[sl, :] = der * pc[sl, :]
     each_group(W, group2)
-    channel_mix(wide(p2), h, W, pw, W)
+    channel_mix(w["point"], h, W, pw, W)
     coef = analyse(h, W, g, waves_ref)
     synthesise(unmix_modes(coef, wr, wi, 1, r), W, a, waves_ref)
     def group3(gr):
@@ -234,10 +241,10 @@
             sl = pl.ds(i * W + gr, 8)
             h[sl, :] = d1[sl, :] * (rows[i] + pw[sl, :])
     each_group(W, group3)
-    channel_mix(wide(both1), h, W, pw, CIN)
+    channel_mix(w["out"], h, W, pw, CIN)
     coef = analyse(h, W, g, waves_ref)
     coef = unmix_modes(coef, wr, wi, 0, r)
-    coef = jnp.dot(lift16, coef, precision=HIGHEST, preferred_element_type=F32)
+    coef = jnp.dot(w["lift"], coef, precision=HIGHEST, preferred_element_type=F32)
     synthesise(coef, CIN, a, waves_ref)
     def group4(gr):
         rows = to_rows(waves_of(a, gr))
@@ -525,18 +532,69 @@
     )
 
 
+Y_SIDE = 4
+EDGES = (1, -1, 2, -2)
+RELAY = {1: 0, -1: VARS, 2: 2 * VARS, -2: 2 * VARS + 1}
+PASSED = {-1: 0, 1: 3, -2: 6, 2: 7}
+
+
+def repack(lanes, main, e, buf, first):
+    for dx in (-1, 1):
+        tiles = [None] * 3
+        for kind, ch, rb, _, width, tile, lane in pieces(dx, -e):
+            value = turned(main[ch], lane - (32 * rb if kind == "near" else 64))
+            tiles[tile] = lanes.put(tiles[tile], value, lane, width)
+        for n, value in enumerate(tiles):
+            row = (first + PASSED[dx] + n) * TILE
+            buf[row:row + TILE, :] = value
+    strip = None
+    for ch in range(4):
+        strip = lanes.put(strip, turned(main[ch], 32 * ch - 64), 32 * ch, 32)
+    last = turned(main[4], -64)
+    corner = lanes.mask(0, 32) & (lanes.row >= 4)
+    for dx in (-2, 2):
+        row = (first + PASSED[dx]) * TILE
+        low, high = (turned(strip, 4, axis=0), last) if dx == -2 else (strip, turned(last, 4, axis=0))
+        buf[row:row + TILE, :] = jnp.where(corner, high, low)
+
+
 def kernel(counts, field_hbm, cot_hbm, lift_hbm, spectral_hbm, point_hbm, proj_hbm, waves_hbm, maps_hbm, out_ref,
            field, cot, lift, spectral, point, proj, waves, maps, f, ct, go, pooled, spread_near, spread_far,
-           fwd_out, fwd_in, bwd_out, bwd_in, load_sem, send_sem, recv_sem, *scr):
+           fwd_out, fwd_in, bwd_out, bwd_in, relay_in, relay_out, load_sem, send_sem, recv_sem, to_mid_sem, at_mid_sem,
+           from_mid_sem, *scr):
     gx, gy = lax.axis_index("gx"), lax.axis_index("gy")
     n_gx, n_gy = counts
-
-    def device(dx, dy):
-        return (lax.rem(gx + (dx + n_gx), n_gx), lax.rem(gy + (dy + n_gy), n_gy))
+    half_z = n_gx // 2
+    n_z = 2 * half_z
+    y = lax.rem(gy, Y_SIDE)
+    index = {o: n for n, o in enumerate(AROUND)}
+
+    def device(dx, dy, base=None):
+        bx, by = base or (gx, gy)
+        return (lax.rem(bx + (dx + n_gx), n_gx), lax.rem(by + (dy + n_gy), n_gy))
+
+    def crosses(e):
+        return (y + e < 0) | (y + e >= Y_SIDE)
+
+    def middle(place, sign):
+        px, py = place
+        core, group = lax.rem(px, 2), lax.div(py, Y_SIDE)
+        z = lax.rem(group, 2) * half_z + lax.div(px, 2)
+        step = sign * (n_z // 4)
+        z = lax.rem(z + jnp.where(core == 0, n_z + step, n_z - step), n_z)
+        row = lax.div(group, 2) * (2 * Y_SIDE) + lax.div(z, half_z) * Y_SIDE + lax.rem(py, Y_SIDE)
+        return (2 * lax.rem(z, half_z) + core, row)
+
+    mine, source = middle((gx, gy), 1), middle((gx, gy), -1)
 
     barrier = pltpu.get_barrier_semaphore()
+    pl.semaphore_signal(barrier, inc=1, device_id=source, device_id_type=MESH)
     for dx, dy in AROUND:
-        pl.semaphore_signal(barrier, inc=1, device_id=device(dx, dy), device_id_type=MESH)
+        owner = device(dx, dy)
+        if dy != 0:
+            via, far_one = middle(owner, 1), crosses(dy)
+            owner = tuple(jnp.where(far_one, a, b) for a, b in zip(via, owner))
+        pl.semaphore_signal(barrier, inc=1, device_id=owner, device_id_type=MESH)
     loads = [
         pltpu.make_async_copy(src, dst, load_sem.at[n])
         for n, (src, dst) in enumerate([
@@ -546,16 +604,32 @@
     for copy in loads:
         copy.start()
 
-    def exchange(turn, src, dst):
-        copies = {}
-        for n, (dx, dy) in enumerate(AROUND):
-            sign = -1 if turn == 0 else 1
-            span = pl.ds(START[dx, dy] * TILE, tiles_of(dx, dy) * TILE)
-            copies[dx, dy] = pltpu.make_async_remote_copy(
-                src_ref=src.at[span], dst_ref=dst.at[span], send_sem=send_sem.at[turn, n], recv_sem=recv_sem.at[turn, n],
-                device_id=device(sign * dx, sign * dy), device_id_type=MESH)
-            copies[dx, dy].start()
-        return copies
+    def span(o):
+        return pl.ds(START[o] * TILE, tiles_of(*o) * TILE)
+
+    def direct(turn, src, dst, o):
+        sign = -1 if turn == 0 else 1
+        return pltpu.make_async_remote_copy(
+            src_ref=src.at[span(o)], dst_ref=dst.at[span(o)], send_sem=send_sem.at[turn, index[o]],
+            recv_sem=recv_sem.at[turn, index[o]], device_id=device(sign * o[0], sign * o[1]), device_id_type=MESH)
+
+    def to_middle(e):
+        tiles = tiles_of(0, -e)
+        return pltpu.make_async_remote_copy(
+            src_ref=fwd_out.at[span((0, -e))], dst_ref=relay_in.at[pl.ds(RELAY[e] * TILE, tiles * TILE)],
+            send_sem=to_mid_sem.at[EDGES.index(e)], recv_sem=at_mid_sem.at[EDGES.index(e)], device_id=mine,
+            device_id_type=MESH)
+
+    def from_middle(e, ex):
+        o = (-ex, -e)
+        if abs(e) == 2 or ex == 0:
+            first, ref = RELAY[e], relay_in
+        else:
+            first, ref = PASSED[-ex] + (0 if e == 1 else 8), relay_out
+        return pltpu.make_async_remote_copy(
+            src_ref=ref.at[pl.ds(first * TILE, tiles_of(*o) * TILE)], dst_ref=fwd_in.at[span(o)],
+            send_sem=from_mid_sem.at[EDGES.index(e), ex + 2], recv_sem=recv_sem.at[0, index[o]],
+            device_id=device(ex, e, source), device_id_type=MESH)
 
     lanes = Lanes()
     loads[0].wait()
@@ -567,8 +641,19 @@
     near = [[got[ch * 16 + rb * 8:ch * 16 + rb * 8 + 8, :COLS] for rb in range(2)] for ch in range(VARS)]
     far = [got[80 + ch * 8:80 + ch * 8 + 8, COLS:] for ch in range(VARS)]
     send_tiles(lanes, near, far, fwd_out)
-    pl.semaphore_wait(barrier, len(AROUND))
-    sent = exchange(0, fwd_out, fwd_in)
+    pl.semaphore_wait(barrier, len(AROUND) + 1)
+    for e in EDGES:
+        @pl.when(crosses(e))
+        def _(e=e):
+            to_middle(e).start()
+    for o in AROUND:
+        if o[1] == 0:
+            direct(0, fwd_out, fwd_in, o).start()
+    for dy in EDGES:
+        @pl.when(jnp.logical_not(crosses(-dy)))
+        def _(dy=dy):
+            for dx in (0, -1, 1, -2, 2):
+                direct(0, fwd_out, fwd_in, (dx, dy)).start()
 
     for copy in loads[2:]:
         copy.wait()
@@ -577,17 +662,28 @@
     for v in range(VARS):
         f[pl.ds(v, ROWS, stride=CIN), :] = field[v * ROWS:(v + 1) * ROWS, :]
         ct[pl.ds(v, ROWS, stride=8), :] = cot[v * ROWS:(v + 1) * ROWS, :]
-    prepare(spectral, scr[0], scr[1])
-    for copy in sent.values():
-        copy.wait_recv()
+    setup = network_setup(ct, lift, spectral, point, proj, scr)
+    for e in EDGES:
+        @pl.when(crosses(e))
+        def _(e=e):
+            to_middle(e).wait_recv()
+            from_middle(e, 0).start()
+            if abs(e) == 1:
+                main = [relay_in[(RELAY[e] + ch) * TILE:(RELAY[e] + ch + 1) * TILE, :] for ch in range(VARS)]
+                repack(Lanes(), main, e, relay_out, 0 if e == 1 else 8)
+            for ex in (-1, 1, -2, 2):
+                from_middle(e, ex).start()
+    for o in AROUND:
+        direct(0, fwd_out, fwd_in, o).wait_recv()
     read_windows(lanes, near, far, fwd_in, f)
-    network_grad(f, ct, lift, spectral, point, proj, waves, go, scr, prep=False)
+    network_grad(f, setup, waves, go, scr)
 
     near, far = window_tiles(go)
     send_grads(lanes, near, far, bwd_out)
-    back = exchange(1, bwd_out, bwd_in)
-    for copy in back.values():
-        copy.wait_recv()
+    for o in AROUND:
+        direct(1, bwd_out, bwd_in, o).start()
+    for o in AROUND:
+        direct(1, bwd_out, bwd_in, o).wait_recv()
     n_sum, f_sum = sum_grads(lanes, near, far, bwd_in)
     got = mapped(jnp.concatenate([n_sum, f_sum], axis=0), maps[COLS:, :])
     for k in range(2):
@@ -595,11 +691,23 @@
     for k in range(4):
         spread_far[pl.ds(k, 40, stride=4), :] = got[80:, COLS:]
     for v in range(VARS):
-        span = slice(v * ROWS, (v + 1) * ROWS)
-        out_ref[span, :] = go[pl.ds(v, ROWS, stride=CIN), :] + spread_near[span, :] + spread_far[span, :]
-    for copies in (sent, back):
-        for copy in copies.values():
-            copy.wait_send()
+        rows = slice(v * ROWS, (v + 1) * ROWS)
+        out_ref[rows, :] = go[pl.ds(v, ROWS, stride=CIN), :] + spread_near[rows, :] + spread_far[rows, :]
+    for o in AROUND:
+        if o[1] == 0:
+            direct(0, fwd_out, fwd_in, o).wait_send()
+        direct(1, bwd_out, bwd_in, o).wait_send()
+    for e in EDGES:
+        @pl.when(crosses(e))
+        def _(e=e):
+            to_middle(e).wait_send()
+            for ex in range(-2, 3):
+                from_middle(e, ex).wait_send()
+
+        @pl.when(jnp.logical_not(crosses(-e)))
+        def _(dy=e):
+            for dx in (0, -1, 1, -2, 2):
+                direct(0, fwd_out, fwd_in, (dx, dy)).wait_send()
 
 
 def body(counts, field, cotangent, lift, spectral, pointwise, project):
@@ -617,8 +725,10 @@
             vmem(ROWS * CIN, COLS), vmem(ROWS * 8, COLS), vmem(ROWS * CIN, COLS),
             vmem(80, COLS), vmem(*flat), vmem(*flat),
             vmem(TILES * TILE, COLS), vmem(TILES * TILE, COLS), vmem(TILES * TILE, COLS), vmem(TILES * TILE, COLS),
+            vmem(12 * TILE, COLS), vmem(16 * TILE, COLS),
             pltpu.SemaphoreType.DMA((8,)), pltpu.SemaphoreType.DMA((2, len(AROUND))),
             pltpu.SemaphoreType.DMA((2, len(AROUND))),
+            pltpu.SemaphoreType.DMA((4,)), pltpu.SemaphoreType.DMA((4,)), pltpu.SemaphoreType.DMA((4, 5)),
             vmem(2, W, W, COLS), vmem(2, W, W, COLS), vmem(W, NWAVE * COLS), vmem(W, NWAVE * COLS),
             vmem(2 * W, COLS), vmem(W * 8, COLS), vmem(ROWS * W, COLS), vmem(ROWS * W, COLS), vmem(ROWS * W, COLS),
             vmem(ROWS * W, COLS),

time: 52.9 us -> 50 us (0.945)
  the two profiles are of different devices: /device:TPU:41 before, /device:TPU:1 now
where the time goes in v2:
time: 50 us; the launch traced here: 49.9 us
  Pallas kernels  49.2 us (98%)
  local copies, waits for them, and re-layouts  0.64 us (1%)
    pallas_call x1, Pallas kernels, body(): call(field.reshape(flat), cotangent.reshape(flat), lift, spectral.transpo...  49.2 us

profile of v2, /device:TPU:1, one launch (start us, length us, event | category | flops | bytes accessed | tf_op | source)
XLA Modules:
  0.0 49.9 jit_solution(6926631195561053520)
XLA Ops:
  0.0 49.2 %patch_grad.1 = f32[160,128]{1,0:T(8,128)S(1)} custom-call(f32[160,128]{1,0:T(8,128)} %bitcast.9, f32[160,128]{1,0:T(8,128)} %bitcast.10, f32[15,32]{1,0:T(8,128)} %lift_hbm.1, f32[2,2,32,32,64]{4,3,2,1,0:T(8,128)} %bitcast.8, f32[2,32,32]{2,1,0:T(8,128)} %point_hbm.1, f32[5,32]{1,0:T(8,128)} %bitcast.11, bf16[1152,256]{1,0:T(8,128)(2,1)} %constant.4.clone.waves_hbm, ...), custom_call_target="tpu_custom_call" | custom-call | tf_op jit(solution)/shard_map/patch_grad/pallas_call | solution.py:739
  49.3 0.6 %copy.11 = f32[5,1,32,128]{3,2,1,0:T(8,128)} copy(f32[5,1,32,128]{3,2,1,0:T(8,128)S(1)} %bitcast.7) | data formatting | bytes 163840

commit v3 on v2

--- a/solution.py
+++ b/solution.py
@@ -263,6 +263,9 @@
 )
 
 
+ROUND = [o for o in AROUND if o[0] > 0]
+
+
 def tiles_of(dx, dy):
     if abs(dx) == 2 or abs(dy) == 2:
         return 1
@@ -561,9 +564,17 @@
 def kernel(counts, field_hbm, cot_hbm, lift_hbm, spectral_hbm, point_hbm, proj_hbm, waves_hbm, maps_hbm, out_ref,
            field, cot, lift, spectral, point, proj, waves, maps, f, ct, go, pooled, spread_near, spread_far,
            fwd_out, fwd_in, bwd_out, bwd_in, relay_in, relay_out, load_sem, send_sem, recv_sem, to_mid_sem, at_mid_sem,
-           from_mid_sem, *scr):
+           from_mid_sem, stage_in, stage_sem, ready_sem, *scr):
     gx, gy = lax.axis_index("gx"), lax.axis_index("gy")
     n_gx, n_gy = counts
+    loads = [
+        pltpu.make_async_copy(src, dst, load_sem.at[n])
+        for n, (src, dst) in enumerate([
+            (field_hbm, field), (maps_hbm, maps), (cot_hbm, cot), (lift_hbm, lift), (point_hbm, point),
+            (proj_hbm, proj), (spectral_hbm, spectral), (waves_hbm, waves)])
+    ]
+    for copy in loads:
+        copy.start()
     half_z = n_gx // 2
     n_z = 2 * half_z
     y = lax.rem(gy, Y_SIDE)
@@ -587,23 +598,70 @@
 
     mine, source = middle((gx, gy), 1), middle((gx, gy), -1)
 
+    hop = 2 * ((half_z - 1) // 2)
+    staged = lax.div(gx, 2) == hop // 2
+    stage_source = gx - hop
+    edge = gx < 2
+
+    def stage_of(px):
+        return px + hop
+
+    def goes_round(o, px):
+        round_end = px - o[0] < 0
+        return round_end if o[1] == 0 else round_end & jnp.logical_not(crosses(-o[1]))
+
+    def count(flag):
+        return jnp.where(flag, 1, 0)
+
+    quarter_z, half_here = n_z // 4, lax.rem(lax.div(gy, Y_SIDE), 2)
+    early_here = half_here * half_z + lax.div(gx, 2) < quarter_z
+    early, tell_later = {}, {}
+    for dx in range(-2, 3):
+        ox = lax.rem(gx + (dx + n_gx), n_gx)
+        oz = (1 - half_here) * half_z + lax.div(ox, 2)
+        oz += jnp.where(lax.rem(ox, 2) == 0, n_z + quarter_z, n_z - quarter_z)
+        early[dx] = lax.rem(oz, n_z) < quarter_z
+
     barrier = pltpu.get_barrier_semaphore()
-    pl.semaphore_signal(barrier, inc=1, device_id=source, device_id_type=MESH)
+    by_middle = half_here == 0
+    relays = lax.rem(lax.div(source[1], Y_SIDE), 2) == 0
+    pl.when(relays)(functools.partial(
+        pl.semaphore_signal, barrier, inc=1, device_id=source, device_id_type=MESH))
     for dx, dy in AROUND:
-        owner = device(dx, dy)
-        if dy != 0:
-            via, far_one = middle(owner, 1), crosses(dy)
-            owner = tuple(jnp.where(far_one, a, b) for a, b in zip(via, owner))
-        pl.semaphore_signal(barrier, inc=1, device_id=owner, device_id_type=MESH)
-    loads = [
-        pltpu.make_async_copy(src, dst, load_sem.at[n])
-        for n, (src, dst) in enumerate([
-            (field_hbm, field), (maps_hbm, maps), (cot_hbm, cot), (lift_hbm, lift), (point_hbm, point),
-            (proj_hbm, proj), (spectral_hbm, spectral), (waves_hbm, waves)])
-    ]
-    for copy in loads:
-        copy.start()
-
+        owner = sender = device(dx, dy)
+        if dx != 0:
+            round_end = gx + dx >= n_gx
+            sender = (jnp.where(round_end, stage_of(owner[0]), owner[0]), owner[1])
+        told = functools.partial(pl.semaphore_signal, barrier, inc=1, device_id_type=MESH)
+        if dy == 0:
+            told(device_id=sender)
+            continue
+        via, far_one = middle(owner, 1), crosses(dy)
+        across = tuple(jnp.where(half_here == 1, a, b) for a, b in zip(via, owner))
+        sender = tuple(jnp.where(far_one, a, b) for a, b in zip(across, sender))
+        tell_later[dx, dy] = (far_one & (half_here == 1) & early[dx], via)
+        pl.when(jnp.logical_not(tell_later[dx, dy][0]))(functools.partial(told, device_id=sender))
+
+    @pl.when(early_here & relays)
+    def _():
+        for e in EDGES:
+            @pl.when(crosses(e))
+            def _(e=e):
+                for ex in range(-2, 3):
+                    pl.semaphore_signal(barrier, inc=1, device_id=device(ex, e, source), device_id_type=MESH)
+
+    @pl.when(staged)
+    def _():
+        pl.semaphore_signal(barrier, inc=1, device_id=(stage_source, gy), device_id_type=MESH)
+
+    expected = len(AROUND) + count(by_middle) + count(edge)
+    for o in AROUND:
+        if o[0] > 0:
+            expected += count(staged & goes_round(o, stage_source)) - count(goes_round(o, gx))
+    for later, _ in tell_later.values():
+        expected += count(later)
+    for e in EDGES:
+        expected += 5 * (count(crosses(e) & relays & jnp.logical_not(early_here)) - count(crosses(e) & by_middle))
     def span(o):
         return pl.ds(START[o] * TILE, tiles_of(*o) * TILE)
 
@@ -631,6 +689,16 @@
             send_sem=from_mid_sem.at[EDGES.index(e), ex + 2], recv_sem=recv_sem.at[0, index[o]],
             device_id=device(ex, e, source), device_id_type=MESH)
 
+    def to_stage(o):
+        return pltpu.make_async_remote_copy(
+            src_ref=fwd_out.at[span(o)], dst_ref=stage_in.at[span(o)], send_sem=stage_sem.at[0, index[o]],
+            recv_sem=stage_sem.at[1, index[o]], device_id=(stage_of(gx), gy), device_id_type=MESH)
+
+    def from_stage(o):
+        return pltpu.make_async_remote_copy(
+            src_ref=stage_in.at[span(o)], dst_ref=fwd_in.at[span(o)], send_sem=stage_sem.at[2, index[o]],
+            recv_sem=recv_sem.at[0, index[o]], device_id=device(-o[0], -o[1], (stage_source, gy)), device_id_type=MESH)
+
     lanes = Lanes()
     loads[0].wait()
     loads[1].wait()
@@ -641,19 +709,36 @@
     near = [[got[ch * 16 + rb * 8:ch * 16 + rb * 8 + 8, :COLS] for rb in range(2)] for ch in range(VARS)]
     far = [got[80 + ch * 8:80 + ch * 8 + 8, COLS:] for ch in range(VARS)]
     send_tiles(lanes, near, far, fwd_out)
-    pl.semaphore_wait(barrier, len(AROUND) + 1)
+    pl.semaphore_wait(barrier, expected)
+    for o, (later, via) in tell_later.items():
+        pl.when(later)(functools.partial(
+            pl.semaphore_signal, ready_sem.at[index[o]], inc=1, device_id=via, device_id_type=MESH))
+
+    def pass_on(e, ex):
+        pl.when(early_here)(functools.partial(pl.semaphore_wait, ready_sem.at[index[-ex, -e]], 1))
+        from_middle(e, ex).start()
+
     for e in EDGES:
-        @pl.when(crosses(e))
+        @pl.when(crosses(e) & by_middle)
         def _(e=e):
             to_middle(e).start()
+    for o in ROUND:
+        @pl.when(goes_round(o, gx))
+        def _(o=o):
+            to_stage(o).start()
+
+    def goes_directly(o):
+        target = gx - o[0]
+        inside = target >= 0
+        if o[1] == 0:
+            return inside
+        across = crosses(-o[1])
+        return (across & jnp.logical_not(by_middle)) | (inside & jnp.logical_not(across))
+
     for o in AROUND:
-        if o[1] == 0:
+        @pl.when(goes_directly(o))
+        def _(o=o):
             direct(0, fwd_out, fwd_in, o).start()
-    for dy in EDGES:
-        @pl.when(jnp.logical_not(crosses(-dy)))
-        def _(dy=dy):
-            for dx in (0, -1, 1, -2, 2):
-                direct(0, fwd_out, fwd_in, (dx, dy)).start()
 
     for copy in loads[2:]:
         copy.wait()
@@ -663,16 +748,26 @@
         f[pl.ds(v, ROWS, stride=CIN), :] = field[v * ROWS:(v + 1) * ROWS, :]
         ct[pl.ds(v, ROWS, stride=8), :] = cot[v * ROWS:(v + 1) * ROWS, :]
     setup = network_setup(ct, lift, spectral, point, proj, scr)
+
+    @pl.when(staged)
+    def _():
+        for o in ROUND:
+            @pl.when(goes_round(o, stage_source))
+            def _(o=o):
+                to_stage(o).wait_recv()
+                from_stage(o).start()
+
     for e in EDGES:
-        @pl.when(crosses(e))
+        @pl.when(crosses(e) & relays)
         def _(e=e):
             to_middle(e).wait_recv()
-            from_middle(e, 0).start()
+            pass_on(e, 0)
             if abs(e) == 1:
                 main = [relay_in[(RELAY[e] + ch) * TILE:(RELAY[e] + ch + 1) * TILE, :] for ch in range(VARS)]
                 repack(Lanes(), main, e, relay_out, 0 if e == 1 else 8)
             for ex in (-1, 1, -2, 2):
-                from_middle(e, ex).start()
+                pass_on(e, ex)
+
     for o in AROUND:
         direct(0, fwd_out, fwd_in, o).wait_recv()
     read_windows(lanes, near, far, fwd_in, f)
@@ -694,20 +789,26 @@
         rows = slice(v * ROWS, (v + 1) * ROWS)
         out_ref[rows, :] = go[pl.ds(v, ROWS, stride=CIN), :] + spread_near[rows, :] + spread_far[rows, :]
     for o in AROUND:
-        if o[1] == 0:
+        direct(1, bwd_out, bwd_in, o).wait_send()
+
+        @pl.when(goes_directly(o))
+        def _(o=o):
             direct(0, fwd_out, fwd_in, o).wait_send()
-        direct(1, bwd_out, bwd_in, o).wait_send()
     for e in EDGES:
-        @pl.when(crosses(e))
+        pl.when(crosses(e) & by_middle)(to_middle(e).wait_send)
+
+        @pl.when(crosses(e) & relays)
         def _(e=e):
-            to_middle(e).wait_send()
             for ex in range(-2, 3):
                 from_middle(e, ex).wait_send()
-
-        @pl.when(jnp.logical_not(crosses(-e)))
-        def _(dy=e):
-            for dx in (0, -1, 1, -2, 2):
-                direct(0, fwd_out, fwd_in, (dx, dy)).wait_send()
+    for o in ROUND:
+        @pl.when(goes_round(o, gx))
+        def _(o=o):
+            to_stage(o).wait_send()
+
+        @pl.when(staged & goes_round(o, stage_source))
+        def _(o=o):
+            from_stage(o).wait_send()
 
 
 def body(counts, field, cotangent, lift, spectral, pointwise, project):
@@ -729,6 +830,8 @@
             pltpu.SemaphoreType.DMA((8,)), pltpu.SemaphoreType.DMA((2, len(AROUND))),
             pltpu.SemaphoreType.DMA((2, len(AROUND))),
             pltpu.SemaphoreType.DMA((4,)), pltpu.SemaphoreType.DMA((4,)), pltpu.SemaphoreType.DMA((4, 5)),
+            vmem(TILES * TILE, COLS), pltpu.SemaphoreType.DMA((3, len(AROUND))),
+            pltpu.SemaphoreType.REGULAR((len(AROUND),)),
             vmem(2, W, W, COLS), vmem(2, W, W, COLS), vmem(W, NWAVE * COLS), vmem(W, NWAVE * COLS),
             vmem(2 * W, COLS), vmem(W * 8, COLS), vmem(ROWS * W, COLS), vmem(ROWS * W, COLS), vmem(ROWS * W, COLS),
             vmem(ROWS * W, COLS),

time: 50 us -> 49.3 us (0.986)
  Pallas kernels: 49.2 us -> 48.5 us
    pallas_call x1, Pallas kernels: 49.2 us -> 48.5 us  [body(): call(field.reshape(flat), cotangent.reshape(flat), lift, spectral.transpo...]
where the time goes in v3:
time: 49.3 us; the launch traced here: 49.2 us
  Pallas kernels  48.5 us (98%)
  local copies, waits for them, and re-layouts  0.64 us (1%)
    pallas_call x1, Pallas kernels, body(): call(field.reshape(flat), cotangent.reshape(flat), lift, spectral.transpo...  48.5 us

profile of v3, /device:TPU:1, one launch (start us, length us, event | category | flops | bytes accessed | tf_op | source)
XLA Modules:
  0.0 49.2 jit_solution(11826654901067454352)
XLA Ops:
  0.0 48.5 %patch_grad.1 = f32[160,128]{1,0:T(8,128)S(1)} custom-call(f32[160,128]{1,0:T(8,128)} %bitcast.9, f32[160,128]{1,0:T(8,128)} %bitcast.10, f32[15,32]{1,0:T(8,128)} %lift_hbm.1, f32[2,2,32,32,64]{4,3,2,1,0:T(8,128)} %bitcast.8, f32[2,32,32]{2,1,0:T(8,128)} %point_hbm.1, f32[5,32]{1,0:T(8,128)} %bitcast.11, bf16[1152,256]{1,0:T(8,128)(2,1)} %constant.4.clone.waves_hbm, ...), custom_call_target="tpu_custom_call" | custom-call | tf_op jit(solution)/shard_map/patch_grad/pallas_call | solution.py:842
  48.5 0.6 %copy.11 = f32[5,1,32,128]{3,2,1,0:T(8,128)} copy(f32[5,1,32,128]{3,2,1,0:T(8,128)S(1)} %bitcast.7) | data formatting | bytes 163840

commit v4 on v3

--- a/solution.py
+++ b/solution.py
@@ -203,7 +203,7 @@
     channel_mix(wide(proj_t), cot_ref, 8, scr[-1], W)
     return {
         "in": wide(both1_t), "out": wide(both1), "point": wide(p2), "point_t": wide(jnp.transpose(p2)),
-        "lift": lift16, "lift_t": lift_t,
+        "lift": wide(lift16), "lift_t": wide(lift_t),
     }
 
 
@@ -212,7 +212,7 @@
     w = setup
     channel_mix(w["in"], f_ref, CIN, pw, W)
     coef = analyse(f_ref, CIN, g, waves_ref)
-    coef = jnp.dot(w["lift_t"], coef, precision=HIGHEST, preferred_element_type=F32)
+    coef = jnp.dot(w["lift_t"], tall(coef), preferred_element_type=F32)
     synthesise(mix_modes(coef, wr, wi, 0, c), W, a, waves_ref)
     def group1(gr):
         rows = to_rows(waves_of(a, gr))
@@ -244,7 +244,7 @@
     channel_mix(w["out"], h, W, pw, CIN)
     coef = analyse(h, W, g, waves_ref)
     coef = unmix_modes(coef, wr, wi, 0, r)
-    coef = jnp.dot(w["lift"], coef, precision=HIGHEST, preferred_element_type=F32)
+    coef = jnp.dot(w["lift"], tall(coef), preferred_element_type=F32)
     synthesise(coef, CIN, a, waves_ref)
     def group4(gr):
         rows = to_rows(waves_of(a, gr))
@@ -465,8 +465,8 @@
     return near, far
 
 
-def send_grads(lanes, near, far, buf):
-    for dx, dy in AROUND:
+def send_grads(lanes, near, far, buf, owners):
+    for dx, dy in owners:
         start = START[dx, dy]
         if abs(dy) == 2:
             tile = None
@@ -774,9 +774,10 @@
     network_grad(f, setup, waves, go, scr)
 
     near, far = window_tiles(go)
-    send_grads(lanes, near, far, bwd_out)
-    for o in AROUND:
-        direct(1, bwd_out, bwd_in, o).start()
+    for owners in ([o for o in AROUND if o[1] != 0], [o for o in AROUND if o[1] == 0]):
+        send_grads(lanes, near, far, bwd_out, owners)
+        for o in owners:
+            direct(1, bwd_out, bwd_in, o).start()
     for o in AROUND:
         direct(1, bwd_out, bwd_in, o).wait_recv()
     n_sum, f_sum = sum_grads(lanes, near, far, bwd_in)

time: 49.3 us -> 49.3 us (level)
  no operation moved by 1% of the time
where the time goes in v4:
time: 49.3 us; the launch traced here: 49.1 us
  Pallas kernels  48.5 us (98%)
  local copies, waits for them, and re-layouts  0.64 us (1%)
    pallas_call x1, Pallas kernels, body(): call(field.reshape(flat), cotangent.reshape(flat), lift, spectral.transpo...  48.5 us

profile of v4, /device:TPU:1, one launch (start us, length us, event | category | flops | bytes accessed | tf_op | source)
XLA Modules:
  0.0 49.1 jit_solution(5018403913076722668)
XLA Ops:
  0.0 48.5 %patch_grad.1 = f32[160,128]{1,0:T(8,128)S(1)} custom-call(f32[160,128]{1,0:T(8,128)} %bitcast.9, f32[160,128]{1,0:T(8,128)} %bitcast.10, f32[15,32]{1,0:T(8,128)} %lift_hbm.1, f32[2,2,32,32,64]{4,3,2,1,0:T(8,128)} %bitcast.8, f32[2,32,32]{2,1,0:T(8,128)} %point_hbm.1, f32[5,32]{1,0:T(8,128)} %bitcast.11, bf16[1152,256]{1,0:T(8,128)(2,1)} %constant.4.clone.waves_hbm, ...), custom_call_target="tpu_custom_call" | custom-call | tf_op jit(solution)/shard_map/patch_grad/pallas_call | solution.py:843
  48.5 0.6 %copy.11 = f32[5,1,32,128]{3,2,1,0:T(8,128)} copy(f32[5,1,32,128]{3,2,1,0:T(8,128)S(1)} %bitcast.7) | data formatting | bytes 163840

commit v5 on v3

--- a/solution.py
+++ b/solution.py
@@ -500,13 +500,18 @@
                 buf[(start + n) * TILE:(start + n + 1) * TILE, :] = value
 
 
-def sum_grads(lanes, near, far, buf):
+def sum_grads(lanes, near, far, buf, wait):
     n_sum = {(ch, rb): lanes.only(near[ch, 1 + rb], 32, 64) for ch in range(VARS) for rb in range(2)}
     f_sum = {ch: lanes.only(far[ch, 0], 48, 32) for ch in range(VARS)}
-    for dx in (-1, 0, 1):
-        for dy in (-1, 0, 1):
+    for o in AROUND:
+        if o[1] == 0:
+            wait(o)
+    for dy in (0, -1, 1):
+        for dx in (-1, 0, 1):
             if (dx, dy) == (0, 0):
                 continue
+            if dy != 0:
+                wait((dx, dy))
             for kind, ch, rb, col, width, tile, lane in pieces(dx, dy):
                 value = tile_at(buf, (dx, dy), tile)
                 if kind == "near":
@@ -515,6 +520,9 @@
                 else:
                     to = far_lane(col)
                     f_sum[ch] += lanes.only(turned(value, to - lane), to, width)
+    for o in AROUND:
+        if o[1] != 0 and max(abs(o[0]), abs(o[1])) == 2:
+            wait(o)
     for dx in (-2, 2):
         value = tree_sum([tile_at(buf, (dx, dy)) for dy in (-1, 0, 1)])
         low = turned(value, 4, axis=0)
@@ -777,9 +785,7 @@
     send_grads(lanes, near, far, bwd_out)
     for o in AROUND:
         direct(1, bwd_out, bwd_in, o).start()
-    for o in AROUND:
-        direct(1, bwd_out, bwd_in, o).wait_recv()
-    n_sum, f_sum = sum_grads(lanes, near, far, bwd_in)
+    n_sum, f_sum = sum_grads(lanes, near, far, bwd_in, lambda o: direct(1, bwd_out, bwd_in, o).wait_recv())
     got = mapped(jnp.concatenate([n_sum, f_sum], axis=0), maps[COLS:, :])
     for k in range(2):
         spread_near[pl.ds(k, 80, stride=2), :] = got[:80, :COLS]

time: 49.3 us -> 49.3 us (level)
  no operation moved by 1% of the time
where the time goes in v5:
time: 49.3 us; the launch traced here: 49.2 us
  Pallas kernels  48.5 us (98%)
  local copies, waits for them, and re-layouts  0.64 us (1%)
    pallas_call x1, Pallas kernels, body(): call(field.reshape(flat), cotangent.reshape(flat), lift, spectral.transpo...  48.5 us

profile of v5, /device:TPU:1, one launch (start us, length us, event | category | flops | bytes accessed | tf_op | source)
XLA Modules:
  0.0 49.2 jit_solution(12908415051265921094)
XLA Ops:
  0.0 48.5 %patch_grad.1 = f32[160,128]{1,0:T(8,128)S(1)} custom-call(f32[160,128]{1,0:T(8,128)} %bitcast.9, f32[160,128]{1,0:T(8,128)} %bitcast.10, f32[15,32]{1,0:T(8,128)} %lift_hbm.1, f32[2,2,32,32,64]{4,3,2,1,0:T(8,128)} %bitcast.8, f32[2,32,32]{2,1,0:T(8,128)} %point_hbm.1, f32[5,32]{1,0:T(8,128)} %bitcast.11, bf16[1152,256]{1,0:T(8,128)(2,1)} %constant.4.clone.waves_hbm, ...), custom_call_target="tpu_custom_call" | custom-call | tf_op jit(solution)/shard_map/patch_grad/pallas_call | solution.py:848
  48.5 0.6 %copy.11 = f32[5,1,32,128]{3,2,1,0:T(8,128)} copy(f32[5,1,32,128]{3,2,1,0:T(8,128)S(1)} %bitcast.7) | data formatting | bytes 163840
